TPU v7x, 32 devices: a whole 2x2x4 slice. The times are simulated.
32 devices in a mesh: row: 8 (over z, y), col: 4 (over x, core).
Axes of the slice: x: 2, y: 2, z: 4, core: 2. Of those that a mesh axis runs over, the one named last changes fastest.
Arguments:
- right_side: float32 [3, 64, 512], P(None, 'row', 'col'), may hold values from -6 to 6
- viscosity: float32 [64, 512], P('row', 'col'), may hold values from 0.1 to 3
- free_mask: int32 [3, 64, 512], P(None, 'row', 'col'), may hold values 0 or 1
- coarse_basis: float32 [64, 3, 64, 512], P(None, None, 'row', 'col'), may hold values from -6 to 6
- gram_inverse: float32 [64, 64], P('col'), may hold values from -3 to 6, as said below
Outputs:
- solution: float32 [3, 64, 512], P(None, 'row', 'col')
- residual: float32 [3, 64, 512], P(None, 'row', 'col')
Inputs may be any that keep to these rules, and one draw needn't show every extreme that they name: `free_mask`: 1 marks a free velocity unknown, 0 one whose value is prescribed. `gram_inverse`: symmetric positive definite.
All inputs are finite; a program needn't handle non-finite values. No bound on the sum of `free_mask` on one device may be relied on, other than what follows from the above.
Results may differ from a plain program's by a relative error of at most 0.0003.
Values sent between devices are 32-bit elements; how exact they have to be, the bound alone decides.
A program may use at most 64 MiB of HBM per device.

v0:
```python
import functools
import math

import jax
import jax.numpy as jnp
from jax import lax
from jax.experimental import pallas as pl
from jax.experimental.pallas import tpu as pltpu
from jax.sharding import PartitionSpec as P

MESH = pl.DeviceIdType.MESH
HIGH = lax.Precision.HIGHEST
F32 = jnp.float32
OPPOSITE = (1, 0, 3, 2)


def zigzag(n):
    order = []
    for i in range(1, n // 2 + 1):
        order += [i, n - i] if 2 * i != n else [i]
    return order


def kernel(
    nrow,
    ncol,
    scale,
    r_hbm,
    visc_hbm,
    mask_hbm,
    basis_ref,
    gram_hbm,
    out_ref,
    r_ref,
    visc_ref,
    mask_ref,
    gram_ref,
    basis_t,
    row_recv,
    col_send,
    col_recv,
    edge_send,
    edge_recv,
    gram_full,
    sum_send,
    sum_recv,
    load_sem,
    small_sem,
    row_ssem,
    row_rsem,
    col_ssem,
    col_rsem,
    edge_ssem,
    edge_rsem,
    gram_ssem,
    gram_rsem,
    sum_ssem,
    sum_rsem,
):
    comps, rows, lanes = r_ref.shape
    basis = basis_ref.shape[0]
    cells = comps * rows
    n = nrow * ncol
    my_row, my_col = lax.axis_index("row"), lax.axis_index("col")
    me = my_row * ncol + my_col
    has = (my_row < nrow - 1, my_row > 0, my_col < ncol - 1, my_col > 0)
    where_to = (
        (my_row + 1, my_col),
        (my_row - 1, my_col),
        (my_row, my_col + 1),
        (my_row, my_col - 1),
    )

    loads = [
        pltpu.make_async_copy(
            basis_ref.at[:, c, r], basis_t.at[c, r], load_sem
        )
        for c in range(comps)
        for r in range(rows)
    ]
    small = [
        pltpu.make_async_copy(src, dst, small_sem.at[i])
        for i, (src, dst) in enumerate(
            (
                (r_hbm, r_ref),
                (visc_hbm, visc_ref),
                (mask_hbm, mask_ref),
                (gram_hbm, gram_ref),
            )
        )
    ]
    for load in small + loads:
        load.start()

    barrier = pltpu.get_barrier_semaphore()

    def to_all(act):
        def one(i, carry):
            t = lax.rem(me + i, n)
            act((t // ncol, lax.rem(t, ncol)))
            return carry

        if n <= 64:
            for i in zigzag(n):
                one(i, 0)
        else:
            lax.fori_loop(1, n, one, 0)

    to_all(
        lambda device: pl.semaphore_signal(
            barrier, inc=1, device_id=device, device_id_type=MESH
        )
    )

    for d in range(4):

        @pl.when(jnp.logical_not(has[d]))
        def _(d=d):
            for stage in range(3):
                edge_recv[stage, d] = jnp.zeros(edge_recv.shape[2:], F32)
            if d < 2:
                row_recv[d] = jnp.zeros(row_recv.shape[1:], F32)
            else:
                col_recv[d - 2] = jnp.zeros(col_recv.shape[1:], F32)

    lane_of = lax.broadcasted_iota(jnp.int32, (rows, lanes), 1)
    row_of = lax.broadcasted_iota(jnp.int32, (rows, lanes), 0)
    diag_mask = [lane_of == row_of + c * rows for c in range(comps)]
    wide_lane = lax.broadcasted_iota(jnp.int32, (basis, lanes), 1)

    def col_to_row(cols):
        out = None
        for c, col in enumerate(cols):
            term = jnp.sum(
                jnp.where(diag_mask[c], jnp.broadcast_to(col, (rows, lanes)), 0.0),
                axis=0,
                keepdims=True,
            )
            out = term if out is None else out + term
        return out

    def row_to_cols(row):
        wide = jnp.broadcast_to(row, (rows, lanes))
        return [
            jnp.sum(jnp.where(diag_mask[c], wide, 0.0), axis=1, keepdims=True)
            for c in range(comps)
        ]

    def shifted(x, north, south, east, west):
        return (
            jnp.where(row_of == rows - 1, north, pltpu.roll(x, rows - 1, axis=0)),
            jnp.where(row_of == 0, south, pltpu.roll(x, 1, axis=0)),
            jnp.where(lane_of == lanes - 1, east, pltpu.roll(x, lanes - 1, axis=1)),
            jnp.where(lane_of == 0, west, pltpu.roll(x, 1, axis=1)),
        )

    def edge_copy(stage, d):
        return pltpu.make_async_remote_copy(
            src_ref=edge_send.at[stage, d],
            dst_ref=edge_recv.at[stage, OPPOSITE[d]],
            send_sem=edge_ssem.at[stage, d],
            recv_sem=edge_rsem.at[stage, OPPOSITE[d]],
            device_id=where_to[d],
            device_id_type=MESH,
        )

    def edge_arrival(stage, d):
        return pltpu.make_async_remote_copy(
            src_ref=edge_send.at[stage, d],
            dst_ref=edge_recv.at[stage, d],
            send_sem=edge_ssem.at[stage, d],
            recv_sem=edge_rsem.at[stage, d],
            device_id=where_to[d],
            device_id_type=MESH,
        )

    def send_edges(stage):
        for d in range(4):
            pl.when(has[d])(edge_copy(stage, d).start)

    def wait_edges(stage):
        for d in range(4):
            pl.when(has[d])(edge_arrival(stage, d).wait_recv)

    def put_edge(stage, d, x, slot):
        if d < 2:
            at = rows - 1 if d == 0 else 0
            for c, part in enumerate(x):
                edge_send[stage, d, slot + c : slot + c + 1] = part[at : at + 1]
        else:
            at = lanes - 1 if d == 2 else 0
            edge_send[stage, d, slot : slot + 1] = col_to_row(
                [part[:, at : at + 1] for part in x]
            )

    def send_sums(phase, row):
        sum_send[phase] = row
        sum_recv[phase, me] = row

        to_all(
            lambda device: pltpu.make_async_remote_copy(
                src_ref=sum_send.at[phase],
                dst_ref=sum_recv.at[phase, me],
                send_sem=sum_ssem.at[phase],
                recv_sem=sum_rsem.at[phase],
                device_id=device,
                device_id_type=MESH,
            ).start()
        )

    def wait_sums(phase):
        others = sum_recv.at[phase, pl.ds(0, n - 1)]
        pltpu.make_async_copy(others, others, sum_rsem.at[phase]).wait()
        return jnp.sum(sum_recv[phase], axis=0)

    def total_row(blocks, sums):
        if sums:
            pad = jnp.zeros((rows - len(sums), lanes), F32)
            blocks = blocks + [jnp.concatenate(sums + [pad], axis=0)]
        out = None
        for i, block in enumerate(blocks):
            col = jnp.sum(block, axis=1, keepdims=True)
            term = jnp.where(lane_of == row_of + i * rows, col, 0.0)
            out = term if out is None else out + term
        return jnp.sum(out, axis=0, keepdims=True)

    def project(x):
        acc = None
        for c in range(comps):
            for r in range(rows):
                term = basis_t[c, r] * x[c][r : r + 1]
                acc = term if acc is None else acc + term
        return [acc[i : i + rows] for i in range(0, basis, rows)]

    def lift(block, coeffs):
        return jnp.sum(block * coeffs, axis=0, keepdims=True)

    def lift_all(coeffs):
        return [
            jnp.concatenate([lift(basis_t[c, r], coeffs) for r in range(rows)], axis=0)
            for c in range(comps)
        ]

    def inner(xs, ys):
        out = None
        for x, y in zip(xs, ys):
            term = jnp.sum(x * y, axis=0, keepdims=True)
            out = term if out is None else out + term
        return out

    for load in small:
        load.wait()
    gram_full[my_col] = gram_ref[...]
    right = [r_ref[c] for c in range(comps)]
    free = [mask_ref[c].astype(F32) for c in range(comps)]
    visc = visc_ref[...]
    for d in range(4):
        slots = (0, comps, 2 * comps) if d < 2 else (0, 1, 2)
        put_edge(0, d, [visc], slots[2])
        put_edge(0, d, right, slots[0])
        put_edge(0, d, free, slots[1])

    pltpu.make_async_copy(basis_t, basis_t, load_sem).wait()
    first = total_row(project(right), [])

    pl.semaphore_wait(barrier, n - 1)
    send_sums(0, first)
    send_edges(0)

    def row_copy(d, dst):
        return pltpu.make_async_remote_copy(
            src_ref=basis_t.at[:, rows - 1 if d == 0 else 0],
            dst_ref=row_recv.at[dst],
            send_sem=row_ssem.at[d],
            recv_sem=row_rsem.at[dst],
            device_id=where_to[d],
            device_id_type=MESH,
        )

    def col_copy(d, dst):
        return pltpu.make_async_remote_copy(
            src_ref=col_send.at[d - 2],
            dst_ref=col_recv.at[dst - 2],
            send_sem=col_ssem.at[d - 2],
            recv_sem=col_rsem.at[dst - 2],
            device_id=where_to[d],
            device_id_type=MESH,
        )

    for d in range(2):
        pl.when(has[d])(row_copy(d, OPPOSITE[d]).start)

    def gram_copy(i):
        return pltpu.make_async_remote_copy(
            src_ref=gram_ref,
            dst_ref=gram_full.at[my_col],
            send_sem=gram_ssem,
            recv_sem=gram_rsem,
            device_id=(my_row, lax.rem(my_col + i, ncol)),
            device_id_type=MESH,
        )

    for i in range(1, ncol):
        gram_copy(i).start()

    for d in (2, 3):
        at = lanes - 1 if d == 2 else 0
        gathered = jnp.zeros((basis, lanes), F32)
        for c in range(comps):
            for r in range(rows):
                spot = c * rows + r
                turned = pltpu.roll(basis_t[c, r], (spot - at) % lanes, axis=1)
                gathered = jnp.where(wide_lane == spot, turned, gathered)
        col_send[d - 2] = gathered
        pl.when(has[d])(col_copy(d, OPPOSITE[d]).start)

    wait_edges(0)
    visc_halo = [edge_recv[0, d, 2 * comps : 2 * comps + 1] for d in range(2)]
    for d in (2, 3):
        visc_halo.append(row_to_cols(edge_recv[0, d, 2:3])[0])
    faces = [0.5 * (visc + v) for v in shifted(visc, *visc_halo)]
    diagonal = 1.0 + faces[0] + faces[1] + faces[2] + faces[3]
    inverse = 1.0 / diagonal
    scaled = [u * inverse for u in free]
    jacobi = [s + (1.0 - u) for s, u in zip(scaled, free)]
    for d in range(4):
        put_edge(1, d, scaled, 0)
    send_edges(1)

    def operate(x, halo):
        out = []
        for c in range(comps):
            masked = free[c] * x[c]
            around = shifted(masked, *[halo[d][c] for d in range(4)])
            stencil = diagonal * masked - (
                faces[0] * around[0]
                + faces[1] * around[1]
                + faces[2] * around[2]
                + faces[3] * around[3]
            )
            out.append(free[c] * stencil + (1.0 - free[c]) * x[c])
        return out

    def halos(coeffs, step):
        out = []
        for d in range(4):
            if d < 2:
                rows_out = []
                for c in range(comps):
                    res = edge_recv[0, d, c : c + 1]
                    if step is not None:
                        res = res - step * edge_recv[2, d, c : c + 1]
                    rows_out.append(
                        edge_recv[1, d, c : c + 1] * res
                        + edge_recv[0, d, comps + c : comps + c + 1]
                        * lift(row_recv[d, c], coeffs)
                    )
                out.append(rows_out)
            else:
                res = edge_recv[0, d, 0:1]
                if step is not None:
                    res = res - step * edge_recv[2, d, 0:1]
                row = edge_recv[1, d, 0:1] * res + edge_recv[0, d, 1:2] * lift(
                    col_recv[d - 2], coeffs
                )
                out.append(row_to_cols(row))
        return out

    for d in range(4):
        if d < 2:
            pl.when(has[d])(row_copy(d, d).wait_recv)
        else:
            pl.when(has[d])(col_copy(d, d).wait_recv)
    others = gram_full.at[pl.ds(0, ncol - 1)]
    pltpu.make_async_copy(others, others, gram_rsem).wait()
    gram = gram_full[...].reshape(basis, basis)
    wait_edges(1)

    def solve(dot):
        return jnp.sum(gram * dot[:, :basis], axis=1, keepdims=True) * scale

    dot = wait_sums(0)
    coeffs = solve(dot)
    direction = [j * r + b for j, r, b in zip(jacobi, right, lift_all(coeffs))]
    image = operate(direction, halos(coeffs, None))
    for d in range(4):
        put_edge(2, d, image, 0)
    send_edges(2)
    second = total_row(
        project(image), [inner(right, direction), inner(direction, image)]
    )
    send_sums(1, second)
    wait_edges(2)
    sums = wait_sums(1)
    energy = sums[:, basis : basis + 1]
    curve = sums[:, basis + 1 : basis + 2]
    step = energy / curve
    residual = [r - step * w for r, w in zip(right, image)]
    coeffs = solve(dot - step * sums)
    smoothed = [j * r + b for j, r, b in zip(jacobi, residual, lift_all(coeffs))]
    smoothed_image = operate(smoothed, halos(coeffs, step))
    third = total_row(
        [],
        [
            inner(residual, smoothed),
            inner(smoothed, image),
            inner(smoothed, smoothed_image),
        ],
    )
    send_sums(2, third)
    sums = wait_sums(2)
    energy_new = sums[:, 0:1]
    ratio = energy_new / energy
    curve_new = sums[:, 2:3] + ratio * (2.0 * sums[:, 1:2] + ratio * curve)
    step_new = energy_new / curve_new
    for c in range(comps):
        out_ref[c] = step * direction[c] + step_new * (smoothed[c] + ratio * direction[c])
        out_ref[comps + c] = residual[c] - step_new * (smoothed_image[c] + ratio * image[c])

    for phase in range(3):
        sent = sum_recv.at[phase, pl.ds(0, n - 1)]
        pltpu.make_async_copy(sent, sent, sum_ssem.at[phase]).wait()
    others = gram_full.at[pl.ds(0, ncol - 1)]
    pltpu.make_async_copy(others, others, gram_ssem).wait()
    for d in range(4):
        for stage in range(3):
            pl.when(has[d])(edge_copy(stage, d).wait_send)
        if d < 2:
            pl.when(has[d])(row_copy(d, d).wait_send)
        else:
            pl.when(has[d])(col_copy(d, d).wait_send)


def on_device(nrow, ncol, right_side, viscosity, free_mask, coarse_basis, gram_inverse):
    comps, rows, lanes = right_side.shape
    basis = coarse_basis.shape[0]
    n = nrow * ncol
    unknowns = comps * rows * lanes * n * basis
    scale = 1.0 / (32.0 * math.sqrt(float(unknowns)))
    vmem = pl.BlockSpec(memory_space=pltpu.VMEM)
    dma = pltpu.SemaphoreType.DMA
    out = pl.pallas_call(
        functools.partial(kernel, nrow, ncol, scale),
        out_shape=pltpu.VMEM((2 * comps, rows, lanes), F32),
        in_specs=[pl.BlockSpec(memory_space=pltpu.HBM)] * 5,
        out_specs=vmem,
        scratch_shapes=[
            pltpu.VMEM(right_side.shape, F32),
            pltpu.VMEM(viscosity.shape, F32),
            pltpu.VMEM(free_mask.shape, free_mask.dtype),
            pltpu.VMEM(gram_inverse.shape, F32),
            pltpu.VMEM((comps, rows, basis, lanes), F32),
            pltpu.VMEM((2, comps, basis, lanes), F32),
            pltpu.VMEM((2, basis, lanes), F32),
            pltpu.VMEM((2, basis, lanes), F32),
            pltpu.VMEM((3, 4, 8, lanes), F32),
            pltpu.VMEM((3, 4, 8, lanes), F32),
            pltpu.VMEM((ncol,) + gram_inverse.shape, F32),
            pltpu.VMEM((3, 1, lanes), F32),
            pltpu.VMEM((3, n, 1, lanes), F32),
            dma,
            dma((4,)),
            dma((2,)),
            dma((2,)),
            dma((2,)),
            dma((2,)),
            dma((3, 4)),
            dma((3, 4)),
            dma,
            dma,
            dma((3,)),
            dma((3,)),
        ],
        compiler_params=pltpu.CompilerParams(
            collective_id=0, has_side_effects=True, vmem_limit_bytes=60_000_000
        ),
    )(right_side, viscosity, free_mask, coarse_basis, gram_inverse)
    return out[:comps], out[comps:]


def solution(mesh):
    in_specs = (
        P(None, "row", "col"),
        P("row", "col"),
        P(None, "row", "col"),
        P(None, None, "row", "col"),
        P("col", None),
    )
    out_specs = (P(None, "row", "col"), P(None, "row", "col"))
    return jax.shard_map(
        functools.partial(on_device, mesh.shape["row"], mesh.shape["col"]),
        mesh=mesh,
        in_specs=in_specs,
        out_specs=out_specs,
        check_vma=False,
    )
```

profile of v0, /device:TPU:0, one launch (start us, length us, event | category | flops | bytes accessed | tf_op | source)
XLA Modules:
  0.0 26.5 jit_solution(4857018258784604874)
XLA Ops:
  0.6 25.2 %shard_map.68 = f32[6,8,128]{2,1,0:T(8,128)S(1)} custom-call(f32[3,8,128]{2,1,0:T(8,128)} %r_hbm.1, f32[8,128]{1,0:T(8,128)} %visc_hbm.1, s32[3,8,128]{2,1,0:T(8,128)} %mask_hbm.1, f32[64,3,8,128]{3,2,1,0:T(8,128)} %basis_ref.1, f32[16,64]{1,0:T(8,128)} %gram_hbm.1), custom_call_target="tpu_custom_call" | custom-call | tf_op jit(solution)/shard_map/pallas_call | solution.py:442
  25.8 0.6 %fusion = (f32[3,8,128]{2,1,0:T(8,128)}, f32[3,8,128]{2,1,0:T(8,128)}) fusion(f32[6,8,128]{2,1,0:T(8,128)S(1)} %shard_map.68), kind=kLoop, calls=%fused_computation | loop fusion | bytes 49152 | tf_op jit(solution)/shard_map/slice | solution.py:478
where the time goes:
time: 26.7 us; the launch traced here: 26.5 us
  Pallas kernels  25.2 us (94%)
  between operations  0.64 us (2%)
  local copies, waits for them, and re-layouts  0.61 us (2%)
    pallas_call x1, Pallas kernels, on_device(): pl.pallas_call(functools.partial(kernel, nrow, ncol, scale), out_shape=pl...  25.2 us
    slice x1, local copies, waits for them, and re-layouts, on_device(): return (out[:comps], out[comps:])  0.61 us

commit v1 on v0

--- a/solution.py
+++ b/solution.py
@@ -19,6 +19,10 @@
     for i in range(1, n // 2 + 1):
         order += [i, n - i] if 2 * i != n else [i]
     return order
+
+
+def plane_rows(nrow):
+    return max(d for d in range(1, nrow + 1) if nrow % d == 0 and d * d <= nrow)
 
 
 def kernel(
@@ -56,6 +60,7 @@
     gram_rsem,
     sum_ssem,
     sum_rsem,
+    chain_sem,
 ):
     comps, rows, lanes = r_ref.shape
     basis = basis_ref.shape[0]
@@ -106,11 +111,44 @@
         else:
             lax.fori_loop(1, n, one, 0)
 
-    to_all(
-        lambda device: pl.semaphore_signal(
-            barrier, inc=1, device_id=device, device_id_type=MESH
-        )
-    )
+    depth = plane_rows(nrow)
+    planes = nrow // depth
+    group = depth * ncol
+    plane, spot_row = my_row // depth, lax.rem(my_row, depth)
+    mine = spot_row * ncol + my_col
+    above, below = plane < planes - 1, plane > 0
+
+    def greet(device):
+        pl.semaphore_signal(barrier, inc=1, device_id=device, device_id_type=MESH)
+
+    greeted = group - 1
+    near = [(above, depth), (below, -depth)]
+    if depth > 1:
+        near.append((jnp.logical_and(above, spot_row == depth - 1), 1))
+        near.append((jnp.logical_and(below, spot_row == 0), -1))
+    for there, step in near:
+        greeted = greeted + jnp.where(there, 1, 0)
+        pl.when(there)(functools.partial(greet, (my_row + step, my_col)))
+    for i in zigzag(group):
+        t = lax.rem(mine + i, group)
+        greet((plane * depth + t // ncol, lax.rem(t, ncol)))
+
+    def pass_on(way, has_from, has_to, step):
+        pl.when(has_from)(lambda: pl.semaphore_wait(chain_sem.at[way], 1))
+        pl.when(has_to)(
+            lambda: pl.semaphore_signal(
+                chain_sem.at[way],
+                inc=1,
+                device_id=(my_row + step, my_col),
+                device_id_type=MESH,
+            )
+        )
+
+    def pass_up():
+        pass_on(0, below, above, depth)
+
+    def pass_down():
+        pass_on(1, above, below, -depth)
 
     for d in range(4):
 
@@ -193,10 +231,11 @@
                 [part[:, at : at + 1] for part in x]
             )
 
-    def send_sums(phase, row):
+    def keep_sums(phase, row):
         sum_send[phase] = row
         sum_recv[phase, me] = row
 
+    def send_sums(phase):
         to_all(
             lambda device: pltpu.make_async_remote_copy(
                 src_ref=sum_send.at[phase],
@@ -260,13 +299,6 @@
         put_edge(0, d, right, slots[0])
         put_edge(0, d, free, slots[1])
 
-    pltpu.make_async_copy(basis_t, basis_t, load_sem).wait()
-    first = total_row(project(right), [])
-
-    pl.semaphore_wait(barrier, n - 1)
-    send_sums(0, first)
-    send_edges(0)
-
     def row_copy(d, dst):
         return pltpu.make_async_remote_copy(
             src_ref=basis_t.at[:, rows - 1 if d == 0 else 0],
@@ -287,9 +319,6 @@
             device_id_type=MESH,
         )
 
-    for d in range(2):
-        pl.when(has[d])(row_copy(d, OPPOSITE[d]).start)
-
     def gram_copy(i):
         return pltpu.make_async_remote_copy(
             src_ref=gram_ref,
@@ -300,18 +329,34 @@
             device_id_type=MESH,
         )
 
+    pl.semaphore_wait(barrier, greeted)
+    send_edges(0)
+    pltpu.make_async_copy(basis_t, basis_t, load_sem).wait()
+    for d in range(2):
+        pl.when(has[d])(row_copy(d, OPPOSITE[d]).start)
+    keep_sums(0, total_row(project(right), []))
+
+    @pl.when(below)
+    def _():
+        pl.when(jnp.logical_not(above))(pass_down)
+        pass_up()
+        pl.when(above)(pass_down)
+        send_sums(0)
+
+    pl.when(jnp.logical_not(below))(pass_up)
     for i in range(1, ncol):
         gram_copy(i).start()
 
+    lows = highs = jnp.zeros((basis, lanes), F32)
+    for c in range(comps):
+        for r in range(rows):
+            spot = c * rows + r
+            turned = pltpu.roll(basis_t[c, r], spot + 1, axis=1)
+            highs = jnp.where(wide_lane == spot, turned, highs)
+            lows = jnp.where(wide_lane == spot + 1, turned, lows)
+    col_send[0] = highs
+    col_send[1] = pltpu.roll(lows, lanes - 1, axis=1)
     for d in (2, 3):
-        at = lanes - 1 if d == 2 else 0
-        gathered = jnp.zeros((basis, lanes), F32)
-        for c in range(comps):
-            for r in range(rows):
-                spot = c * rows + r
-                turned = pltpu.roll(basis_t[c, r], (spot - at) % lanes, axis=1)
-                gathered = jnp.where(wide_lane == spot, turned, gathered)
-        col_send[d - 2] = gathered
         pl.when(has[d])(col_copy(d, OPPOSITE[d]).start)
 
     wait_edges(0)
@@ -326,6 +371,11 @@
     for d in range(4):
         put_edge(1, d, scaled, 0)
     send_edges(1)
+
+    @pl.when(jnp.logical_not(below))
+    def _():
+        pass_down()
+        send_sums(0)
 
     def operate(x, halo):
         out = []
@@ -389,7 +439,8 @@
     second = total_row(
         project(image), [inner(right, direction), inner(direction, image)]
     )
-    send_sums(1, second)
+    keep_sums(1, second)
+    send_sums(1)
     wait_edges(2)
     sums = wait_sums(1)
     energy = sums[:, basis : basis + 1]
@@ -407,7 +458,8 @@
             inner(smoothed, smoothed_image),
         ],
     )
-    send_sums(2, third)
+    keep_sums(2, third)
+    send_sums(2)
     sums = wait_sums(2)
     energy_new = sums[:, 0:1]
     ratio = energy_new / energy
@@ -470,6 +522,7 @@
             dma,
             dma((3,)),
             dma((3,)),
+            pltpu.SemaphoreType.REGULAR((2,)),
         ],
         compiler_params=pltpu.CompilerParams(
             collective_id=0, has_side_effects=True, vmem_limit_bytes=60_000_000

time: 26.7 us -> 24 us (0.90)
  Pallas kernels: 25.2 us -> 22.5 us
    pallas_call x1, Pallas kernels: 25.2 us -> 22.5 us  [on_device(): pl.pallas_call(functools.partial(kernel, nrow, ncol, scale), out_shape=pl...]
where the time goes in v1:
time: 24 us; the launch traced here: 23.8 us
  Pallas kernels  22.5 us (94%)
  between operations  0.64 us (3%)
  local copies, waits for them, and re-layouts  0.61 us (3%)
    pallas_call x1, Pallas kernels, on_device(): pl.pallas_call(functools.partial(kernel, nrow, ncol, scale), out_shape=pl...  22.5 us
    slice x1, local copies, waits for them, and re-layouts, on_device(): return (out[:comps], out[comps:])  0.61 us

profile of v1, /device:TPU:0, one launch (start us, length us, event | category | flops | bytes accessed | tf_op | source)
XLA Modules:
  0.0 23.8 jit_solution(13228385043966760455)
XLA Ops:
  0.6 22.5 %shard_map.68 = f32[6,8,128]{2,1,0:T(8,128)S(1)} custom-call(f32[3,8,128]{2,1,0:T(8,128)} %r_hbm.1, f32[8,128]{1,0:T(8,128)} %visc_hbm.1, s32[3,8,128]{2,1,0:T(8,128)} %mask_hbm.1, f32[64,3,8,128]{3,2,1,0:T(8,128)} %basis_ref.1, f32[16,64]{1,0:T(8,128)} %gram_hbm.1), custom_call_target="tpu_custom_call" | custom-call | tf_op jit(solution)/shard_map/pallas_call | solution.py:494
  23.2 0.6 %fusion = (f32[3,8,128]{2,1,0:T(8,128)}, f32[3,8,128]{2,1,0:T(8,128)}) fusion(f32[6,8,128]{2,1,0:T(8,128)S(1)} %shard_map.68), kind=kLoop, calls=%fused_computation | loop fusion | bytes 49152 | tf_op jit(solution)/shard_map/slice | solution.py:531

commit v2 on v1

--- a/solution.py
+++ b/solution.py
@@ -12,6 +12,8 @@
 HIGH = lax.Precision.HIGHEST
 F32 = jnp.float32
 OPPOSITE = (1, 0, 3, 2)
+NORTH, SOUTH, EAST, WEST = range(4)
+EVERY = (NORTH, SOUTH, EAST, WEST)
 
 
 def zigzag(n):
@@ -45,6 +47,8 @@
     col_recv,
     edge_send,
     edge_recv,
+    diag_send,
+    diag_recv,
     gram_full,
     sum_send,
     sum_recv,
@@ -56,6 +60,8 @@
     col_rsem,
     edge_ssem,
     edge_rsem,
+    diag_ssem,
+    diag_rsem,
     gram_ssem,
     gram_rsem,
     sum_ssem,
@@ -76,6 +82,12 @@
         (my_row, my_col - 1),
     )
 
+    has_diag = (
+        jnp.logical_and(has[NORTH], has[WEST]),
+        jnp.logical_and(has[SOUTH], has[EAST]),
+    )
+    diag_to = ((my_row + 1, my_col - 1), (my_row - 1, my_col + 1))
+
     loads = [
         pltpu.make_async_copy(
             basis_ref.at[:, c, r], basis_t.at[c, r], load_sem
@@ -121,45 +133,54 @@
     def greet(device):
         pl.semaphore_signal(barrier, inc=1, device_id=device, device_id_type=MESH)
 
-    greeted = group - 1
-    near = [(above, depth), (below, -depth)]
-    if depth > 1:
-        near.append((jnp.logical_and(above, spot_row == depth - 1), 1))
-        near.append((jnp.logical_and(below, spot_row == 0), -1))
-    for there, step in near:
-        greeted = greeted + jnp.where(there, 1, 0)
-        pl.when(there)(functools.partial(greet, (my_row + step, my_col)))
+    cross_down = jnp.logical_and(below, spot_row == 0)
+    cross_up = jnp.logical_and(above, spot_row == depth - 1)
+    greeted = plane * group + group - 1 + jnp.where(cross_up, 1, 0)
+    pl.when(cross_down)(functools.partial(greet, (my_row - 1, my_col)))
+
+    def greet_higher(i, carry):
+        t = (plane + 1) * group + i
+        greet((t // ncol, lax.rem(t, ncol)))
+        return carry
+
+    lax.fori_loop(0, (planes - 1 - plane) * group, greet_higher, 0)
     for i in zigzag(group):
         t = lax.rem(mine + i, group)
         greet((plane * depth + t // ncol, lax.rem(t, ncol)))
 
-    def pass_on(way, has_from, has_to, step):
-        pl.when(has_from)(lambda: pl.semaphore_wait(chain_sem.at[way], 1))
-        pl.when(has_to)(
-            lambda: pl.semaphore_signal(
-                chain_sem.at[way],
+    def tell_lower():
+        def tell(q, carry):
+            pl.semaphore_signal(
+                chain_sem,
                 inc=1,
-                device_id=(my_row + step, my_col),
+                device_id=(q * depth + spot_row, my_col),
                 device_id_type=MESH,
             )
-        )
-
-    def pass_up():
-        pass_on(0, below, above, depth)
-
-    def pass_down():
-        pass_on(1, above, below, -depth)
+            return carry
+
+        lax.fori_loop(0, plane, tell, 0)
+
+    def hear_higher():
+        pl.when(above)(lambda: pl.semaphore_wait(chain_sem, planes - 1 - plane))
+
+    top = jnp.logical_not(above)
 
     for d in range(4):
 
         @pl.when(jnp.logical_not(has[d]))
         def _(d=d):
-            for stage in range(3):
+            for stage in range(4):
                 edge_recv[stage, d] = jnp.zeros(edge_recv.shape[2:], F32)
-            if d < 2:
-                row_recv[d] = jnp.zeros(row_recv.shape[1:], F32)
-            else:
-                col_recv[d - 2] = jnp.zeros(col_recv.shape[1:], F32)
+            if d == SOUTH:
+                row_recv[...] = jnp.zeros(row_recv.shape, F32)
+            if d == WEST:
+                col_recv[...] = jnp.zeros(col_recv.shape, F32)
+
+    for i in range(2):
+
+        @pl.when(jnp.logical_not(has_diag[1 - i]))
+        def _(i=i):
+            diag_recv[i] = jnp.zeros(diag_recv.shape[1:], F32)
 
     lane_of = lax.broadcasted_iota(jnp.int32, (rows, lanes), 1)
     row_of = lax.broadcasted_iota(jnp.int32, (rows, lanes), 0)
@@ -212,24 +233,34 @@
             device_id_type=MESH,
         )
 
-    def send_edges(stage):
-        for d in range(4):
+    def diag_copy(i):
+        return pltpu.make_async_remote_copy(
+            src_ref=diag_send.at[i],
+            dst_ref=diag_recv.at[i],
+            send_sem=diag_ssem.at[i],
+            recv_sem=diag_rsem.at[i],
+            device_id=diag_to[i],
+            device_id_type=MESH,
+        )
+
+    def send_edges(stage, ways):
+        for d in ways:
             pl.when(has[d])(edge_copy(stage, d).start)
 
-    def wait_edges(stage):
-        for d in range(4):
+    def wait_edges(stage, sides):
+        for d in sides:
             pl.when(has[d])(edge_arrival(stage, d).wait_recv)
 
+    def edge_rows(d, x):
+        if d < 2:
+            at = rows - 1 if d == NORTH else 0
+            return [part[at : at + 1] for part in x]
+        at = lanes - 1 if d == EAST else 0
+        return [col_to_row([part[:, at : at + 1] for part in x])]
+
     def put_edge(stage, d, x, slot):
-        if d < 2:
-            at = rows - 1 if d == 0 else 0
-            for c, part in enumerate(x):
-                edge_send[stage, d, slot + c : slot + c + 1] = part[at : at + 1]
-        else:
-            at = lanes - 1 if d == 2 else 0
-            edge_send[stage, d, slot : slot + 1] = col_to_row(
-                [part[:, at : at + 1] for part in x]
-            )
+        for i, row in enumerate(edge_rows(d, x)):
+            edge_send[stage, d, slot + i : slot + i + 1] = row
 
     def keep_sums(phase, row):
         sum_send[phase] = row
@@ -293,31 +324,28 @@
     right = [r_ref[c] for c in range(comps)]
     free = [mask_ref[c].astype(F32) for c in range(comps)]
     visc = visc_ref[...]
-    for d in range(4):
-        slots = (0, comps, 2 * comps) if d < 2 else (0, 1, 2)
-        put_edge(0, d, [visc], slots[2])
-        put_edge(0, d, right, slots[0])
-        put_edge(0, d, free, slots[1])
-
-    def row_copy(d, dst):
-        return pltpu.make_async_remote_copy(
-            src_ref=basis_t.at[:, rows - 1 if d == 0 else 0],
-            dst_ref=row_recv.at[dst],
-            send_sem=row_ssem.at[d],
-            recv_sem=row_rsem.at[dst],
-            device_id=where_to[d],
-            device_id_type=MESH,
-        )
-
-    def col_copy(d, dst):
-        return pltpu.make_async_remote_copy(
-            src_ref=col_send.at[d - 2],
-            dst_ref=col_recv.at[dst - 2],
-            send_sem=col_ssem.at[d - 2],
-            recv_sem=col_rsem.at[dst - 2],
-            device_id=where_to[d],
-            device_id_type=MESH,
-        )
+    for d in EVERY:
+        put_edge(0, d, [visc], 2 * comps if d < 2 else 2)
+    for d in (NORTH, EAST):
+        put_edge(0, d, right, 0)
+        put_edge(0, d, free, comps if d < 2 else 1)
+
+    row_copy = pltpu.make_async_remote_copy(
+        src_ref=basis_t.at[:, rows - 1],
+        dst_ref=row_recv,
+        send_sem=row_ssem,
+        recv_sem=row_rsem,
+        device_id=where_to[NORTH],
+        device_id_type=MESH,
+    )
+    col_copy = pltpu.make_async_remote_copy(
+        src_ref=col_send,
+        dst_ref=col_recv,
+        send_sem=col_ssem,
+        recv_sem=col_rsem,
+        device_id=where_to[EAST],
+        device_id_type=MESH,
+    )
 
     def gram_copy(i):
         return pltpu.make_async_remote_copy(
@@ -330,58 +358,67 @@
         )
 
     pl.semaphore_wait(barrier, greeted)
-    send_edges(0)
+    tell_lower()
+    send_edges(0, EVERY)
     pltpu.make_async_copy(basis_t, basis_t, load_sem).wait()
-    for d in range(2):
-        pl.when(has[d])(row_copy(d, OPPOSITE[d]).start)
+    pl.when(has[NORTH])(row_copy.start)
     keep_sums(0, total_row(project(right), []))
 
-    @pl.when(below)
-    def _():
-        pl.when(jnp.logical_not(above))(pass_down)
-        pass_up()
-        pl.when(above)(pass_down)
-        send_sums(0)
-
-    pl.when(jnp.logical_not(below))(pass_up)
+    pl.when(top)(lambda: send_sums(0))
     for i in range(1, ncol):
         gram_copy(i).start()
 
-    lows = highs = jnp.zeros((basis, lanes), F32)
+    column = jnp.zeros((basis, lanes), F32)
     for c in range(comps):
         for r in range(rows):
             spot = c * rows + r
-            turned = pltpu.roll(basis_t[c, r], spot + 1, axis=1)
-            highs = jnp.where(wide_lane == spot, turned, highs)
-            lows = jnp.where(wide_lane == spot + 1, turned, lows)
-    col_send[0] = highs
-    col_send[1] = pltpu.roll(lows, lanes - 1, axis=1)
-    for d in (2, 3):
-        pl.when(has[d])(col_copy(d, OPPOSITE[d]).start)
-
-    wait_edges(0)
+            turned = pltpu.roll(basis_t[c, r], (spot + 1) % lanes, axis=1)
+            column = jnp.where(wide_lane == spot, turned, column)
+    col_send[...] = column
+    pl.when(has[EAST])(col_copy.start)
+
+    def hear_and_send():
+        hear_higher()
+        send_sums(0)
+
+    pl.when(above)(hear_and_send)
+
+    wait_edges(0, EVERY)
     visc_halo = [edge_recv[0, d, 2 * comps : 2 * comps + 1] for d in range(2)]
-    for d in (2, 3):
+    for d in (EAST, WEST):
         visc_halo.append(row_to_cols(edge_recv[0, d, 2:3])[0])
     faces = [0.5 * (visc + v) for v in shifted(visc, *visc_halo)]
     diagonal = 1.0 + faces[0] + faces[1] + faces[2] + faces[3]
     inverse = 1.0 / diagonal
     scaled = [u * inverse for u in free]
     jacobi = [s + (1.0 - u) for s, u in zip(scaled, free)]
-    for d in range(4):
+    for d in (NORTH, EAST):
         put_edge(1, d, scaled, 0)
-    send_edges(1)
-
-    @pl.when(jnp.logical_not(below))
-    def _():
-        pass_down()
-        send_sums(0)
-
-    def operate(x, halo):
-        out = []
+    send_edges(1, (NORTH, EAST))
+
+    pl.when(has[SOUTH])(row_copy.wait_recv)
+    pl.when(has[WEST])(col_copy.wait_recv)
+    others = gram_full.at[pl.ds(0, ncol - 1)]
+    pltpu.make_async_copy(others, others, gram_rsem).wait()
+    gram = gram_full[...].reshape(basis, basis)
+    wait_edges(1, (SOUTH, WEST))
+    south_right = [edge_recv[0, SOUTH, c : c + 1] for c in range(comps)]
+    south_free = [edge_recv[0, SOUTH, comps + c : comps + c + 1] for c in range(comps)]
+    south_scaled = [edge_recv[1, SOUTH, c : c + 1] for c in range(comps)]
+    west_right, west_free = edge_recv[0, WEST, 0:1], edge_recv[0, WEST, 1:2]
+    west_scaled = edge_recv[1, WEST, 0:1]
+
+    def operate(x, coeffs, south_res, west_res):
+        south = [
+            s * r + u * lift(row_recv[c], coeffs)
+            for c, (s, r, u) in enumerate(zip(south_scaled, south_res, south_free))
+        ]
+        west = west_scaled * west_res + west_free * lift(col_recv[...], coeffs)
+        west_cols = row_to_cols(west)
+        out, to_south, to_west = [], [], []
         for c in range(comps):
             masked = free[c] * x[c]
-            around = shifted(masked, *[halo[d][c] for d in range(4)])
+            around = shifted(masked, 0.0, south[c], 0.0, west_cols[c])
             stencil = diagonal * masked - (
                 faces[0] * around[0]
                 + faces[1] * around[1]
@@ -389,42 +426,35 @@
                 + faces[3] * around[3]
             )
             out.append(free[c] * stencil + (1.0 - free[c]) * x[c])
-        return out
-
-    def halos(coeffs, step):
-        out = []
-        for d in range(4):
-            if d < 2:
-                rows_out = []
-                for c in range(comps):
-                    res = edge_recv[0, d, c : c + 1]
-                    if step is not None:
-                        res = res - step * edge_recv[2, d, c : c + 1]
-                    rows_out.append(
-                        edge_recv[1, d, c : c + 1] * res
-                        + edge_recv[0, d, comps + c : comps + c + 1]
-                        * lift(row_recv[d, c], coeffs)
-                    )
-                out.append(rows_out)
-            else:
-                res = edge_recv[0, d, 0:1]
-                if step is not None:
-                    res = res - step * edge_recv[2, d, 0:1]
-                row = edge_recv[1, d, 0:1] * res + edge_recv[0, d, 1:2] * lift(
-                    col_recv[d - 2], coeffs
-                )
-                out.append(row_to_cols(row))
-        return out
-
-    for d in range(4):
-        if d < 2:
-            pl.when(has[d])(row_copy(d, d).wait_recv)
-        else:
-            pl.when(has[d])(col_copy(d, d).wait_recv)
-    others = gram_full.at[pl.ds(0, ncol - 1)]
-    pltpu.make_async_copy(others, others, gram_rsem).wait()
-    gram = gram_full[...].reshape(basis, basis)
-    wait_edges(1)
+            to_south.append(faces[1] * masked)
+            to_west.append(faces[3] * masked)
+        return out, to_south, to_west, south, west
+
+    def put_terms(stage, to_south, to_west):
+        south_rows = edge_rows(SOUTH, to_south)
+        west_row = edge_rows(WEST, to_west)[0]
+        for c in range(comps):
+            edge_send[stage, SOUTH, c : c + 1] = south_rows[c]
+        edge_send[stage, WEST, 0:1] = west_row
+        return [-u * q for u, q in zip(south_free, south_rows)], -west_free * west_row
+
+    def cross(south, west, south_term, west_term):
+        total = west * west_term
+        for a, b in zip(south, south_term):
+            total = total + a * b
+        return total
+
+    def complete(stage, image):
+        east_cols = row_to_cols(edge_recv[stage, EAST, 0:1])
+        return [
+            image[c]
+            - free[c]
+            * (
+                jnp.where(row_of == rows - 1, edge_recv[stage, NORTH, c : c + 1], 0.0)
+                + jnp.where(lane_of == lanes - 1, east_cols[c], 0.0)
+            )
+            for c in range(comps)
+        ]
 
     def solve(dot):
         return jnp.sum(gram * dot[:, :basis], axis=1, keepdims=True) * scale
@@ -432,16 +462,48 @@
     dot = wait_sums(0)
     coeffs = solve(dot)
     direction = [j * r + b for j, r, b in zip(jacobi, right, lift_all(coeffs))]
-    image = operate(direction, halos(coeffs, None))
-    for d in range(4):
-        put_edge(2, d, image, 0)
-    send_edges(2)
+    image, to_south, to_west, south, west = operate(
+        direction, coeffs, south_right, west_right
+    )
+    south_term, west_term = put_terms(2, to_south, to_west)
+    across = project(image)
+    extra = col_recv[...] * west_term
+    for c in range(comps):
+        extra = extra + row_recv[c] * south_term[c]
+    across = [a + extra[i * rows : (i + 1) * rows] for i, a in enumerate(across)]
     second = total_row(
-        project(image), [inner(right, direction), inner(direction, image)]
+        across,
+        [
+            inner(right, direction),
+            inner(direction, image) + cross(south, west, south_term, west_term),
+        ],
     )
     keep_sums(1, second)
     send_sums(1)
-    wait_edges(2)
+    for d in (NORTH, EAST):
+        put_edge(2, d, image, 0)
+    corner_row = jnp.where(row_of == rows - 1, 1.0, 0.0)
+    turned = [pltpu.roll(q, lanes - 1, axis=1) for q in to_west]
+    for c in range(comps):
+        diag_send[0, c : c + 1] = jnp.where(
+            lane_of == lanes - 1, turned[c], 0.0
+        )[rows - 1 : rows]
+    turned = [pltpu.roll(q, rows - 1, axis=0) * corner_row for q in to_south]
+    diag_send[1, 0:1] = col_to_row([q[:, lanes - 1 : lanes] for q in turned])
+    send_edges(2, EVERY)
+    for i in range(2):
+        pl.when(has_diag[i])(diag_copy(i).start)
+    wait_edges(2, EVERY)
+    for i in range(2):
+        pl.when(has_diag[1 - i])(diag_copy(i).wait_recv)
+    image = complete(2, image)
+    south_image = [
+        edge_recv[2, SOUTH, c : c + 1]
+        + south_term[c]
+        - south_free[c] * diag_recv[0, c : c + 1]
+        for c in range(comps)
+    ]
+    west_image = edge_recv[2, WEST, 0:1] + west_term - west_free * diag_recv[1, 0:1]
     sums = wait_sums(1)
     energy = sums[:, basis : basis + 1]
     curve = sums[:, basis + 1 : basis + 2]
@@ -449,17 +511,27 @@
     residual = [r - step * w for r, w in zip(right, image)]
     coeffs = solve(dot - step * sums)
     smoothed = [j * r + b for j, r, b in zip(jacobi, residual, lift_all(coeffs))]
-    smoothed_image = operate(smoothed, halos(coeffs, step))
+    smoothed_image, to_south, to_west, south, west = operate(
+        smoothed,
+        coeffs,
+        [r - step * w for r, w in zip(south_right, south_image)],
+        west_right - step * west_image,
+    )
+    south_term, west_term = put_terms(3, to_south, to_west)
     third = total_row(
         [],
         [
             inner(residual, smoothed),
             inner(smoothed, image),
-            inner(smoothed, smoothed_image),
+            inner(smoothed, smoothed_image)
+            + cross(south, west, south_term, west_term),
         ],
     )
     keep_sums(2, third)
     send_sums(2)
+    send_edges(3, (SOUTH, WEST))
+    wait_edges(3, (NORTH, EAST))
+    smoothed_image = complete(3, smoothed_image)
     sums = wait_sums(2)
     energy_new = sums[:, 0:1]
     ratio = energy_new / energy
@@ -474,13 +546,13 @@
         pltpu.make_async_copy(sent, sent, sum_ssem.at[phase]).wait()
     others = gram_full.at[pl.ds(0, ncol - 1)]
     pltpu.make_async_copy(others, others, gram_ssem).wait()
-    for d in range(4):
-        for stage in range(3):
+    for stage, ways in enumerate((EVERY, (NORTH, EAST), EVERY, (SOUTH, WEST))):
+        for d in ways:
             pl.when(has[d])(edge_copy(stage, d).wait_send)
-        if d < 2:
-            pl.when(has[d])(row_copy(d, d).wait_send)
-        else:
-            pl.when(has[d])(col_copy(d, d).wait_send)
+    for i in range(2):
+        pl.when(has_diag[i])(diag_copy(i).wait_send)
+    pl.when(has[NORTH])(row_copy.wait_send)
+    pl.when(has[EAST])(col_copy.wait_send)
 
 
 def on_device(nrow, ncol, right_side, viscosity, free_mask, coarse_basis, gram_inverse):
@@ -502,27 +574,31 @@
             pltpu.VMEM(free_mask.shape, free_mask.dtype),
             pltpu.VMEM(gram_inverse.shape, F32),
             pltpu.VMEM((comps, rows, basis, lanes), F32),
-            pltpu.VMEM((2, comps, basis, lanes), F32),
-            pltpu.VMEM((2, basis, lanes), F32),
-            pltpu.VMEM((2, basis, lanes), F32),
-            pltpu.VMEM((3, 4, 8, lanes), F32),
-            pltpu.VMEM((3, 4, 8, lanes), F32),
+            pltpu.VMEM((comps, basis, lanes), F32),
+            pltpu.VMEM((basis, lanes), F32),
+            pltpu.VMEM((basis, lanes), F32),
+            pltpu.VMEM((4, 4, 8, lanes), F32),
+            pltpu.VMEM((4, 4, 8, lanes), F32),
+            pltpu.VMEM((2, 8, lanes), F32),
+            pltpu.VMEM((2, 8, lanes), F32),
             pltpu.VMEM((ncol,) + gram_inverse.shape, F32),
             pltpu.VMEM((3, 1, lanes), F32),
             pltpu.VMEM((3, n, 1, lanes), F32),
             dma,
             dma((4,)),
+            dma,
+            dma,
+            dma,
+            dma,
+            dma((4, 4)),
+            dma((4, 4)),
             dma((2,)),
             dma((2,)),
-            dma((2,)),
-            dma((2,)),
-            dma((3, 4)),
-            dma((3, 4)),
             dma,
             dma,
             dma((3,)),
             dma((3,)),
-            pltpu.SemaphoreType.REGULAR((2,)),
+            pltpu.SemaphoreType.REGULAR,
         ],
         compiler_params=pltpu.CompilerParams(
             collective_id=0, has_side_effects=True, vmem_limit_bytes=60_000_000

time: 24 us -> 22.9 us (0.954)
  Pallas kernels: 22.5 us -> 21.5 us
    pallas_call x1, Pallas kernels: 22.5 us -> 21.5 us  [on_device(): pl.pallas_call(functools.partial(kernel, nrow, ncol, scale), out_shape=pl...]
where the time goes in v2:
time: 22.9 us; the launch traced here: 22.7 us
  Pallas kernels  21.5 us (94%)
  between operations  0.64 us (3%)
  local copies, waits for them, and re-layouts  0.61 us (3%)
    pallas_call x1, Pallas kernels, on_device(): pl.pallas_call(functools.partial(kernel, nrow, ncol, scale), out_shape=pl...  21.5 us
    slice x1, local copies, waits for them, and re-layouts, on_device(): return (out[:comps], out[comps:])  0.61 us

profile of v2, /device:TPU:0, one launch (start us, length us, event | category | flops | bytes accessed | tf_op | source)
XLA Modules:
  0.0 22.7 jit_solution(7317828383631193191)
XLA Ops:
  0.6 21.5 %shard_map.68 = f32[6,8,128]{2,1,0:T(8,128)S(1)} custom-call(f32[3,8,128]{2,1,0:T(8,128)} %r_hbm.1, f32[8,128]{1,0:T(8,128)} %visc_hbm.1, s32[3,8,128]{2,1,0:T(8,128)} %mask_hbm.1, f32[64,3,8,128]{3,2,1,0:T(8,128)} %basis_ref.1, f32[16,64]{1,0:T(8,128)} %gram_hbm.1), custom_call_target="tpu_custom_call" | custom-call | tf_op jit(solution)/shard_map/pallas_call | solution.py:566
  22.1 0.6 %fusion = (f32[3,8,128]{2,1,0:T(8,128)}, f32[3,8,128]{2,1,0:T(8,128)}) fusion(f32[6,8,128]{2,1,0:T(8,128)S(1)} %shard_map.68), kind=kLoop, calls=%fused_computation | loop fusion | bytes 49152 | tf_op jit(solution)/shard_map/slice | solution.py:607

commit v3 on v2

--- a/solution.py
+++ b/solution.py
@@ -14,6 +14,11 @@
 OPPOSITE = (1, 0, 3, 2)
 NORTH, SOUTH, EAST, WEST = range(4)
 EVERY = (NORTH, SOUTH, EAST, WEST)
+SENT = (EVERY, (NORTH, EAST), EVERY, (SOUTH, WEST))
+SENT_AT = {}
+for _stage, _ways in enumerate(SENT):
+    for _way in _ways:
+        SENT_AT[_stage, _way] = len(SENT_AT)
 
 
 def zigzag(n):
@@ -217,21 +222,30 @@
         return pltpu.make_async_remote_copy(
             src_ref=edge_send.at[stage, d],
             dst_ref=edge_recv.at[stage, OPPOSITE[d]],
-            send_sem=edge_ssem.at[stage, d],
-            recv_sem=edge_rsem.at[stage, OPPOSITE[d]],
+            send_sem=edge_ssem.at[SENT_AT[stage, d]],
+            recv_sem=edge_rsem.at[SENT_AT[stage, d]],
             device_id=where_to[d],
             device_id_type=MESH,
         )
 
     def edge_arrival(stage, d):
+        at = SENT_AT[stage, OPPOSITE[d]]
         return pltpu.make_async_remote_copy(
             src_ref=edge_send.at[stage, d],
             dst_ref=edge_recv.at[stage, d],
-            send_sem=edge_ssem.at[stage, d],
-            recv_sem=edge_rsem.at[stage, d],
+            send_sem=edge_ssem.at[at],
+            recv_sem=edge_rsem.at[at],
             device_id=where_to[d],
             device_id_type=MESH,
         )
+
+    def drain_sums(phase):
+        sent = sum_recv.at[phase, pl.ds(0, n - 1)]
+        pltpu.make_async_copy(sent, sent, sum_ssem.at[phase]).wait()
+
+    def drain_edges(stage):
+        for d in SENT[stage]:
+            pl.when(has[d])(edge_copy(stage, d).wait_send)
 
     def diag_copy(i):
         return pltpu.make_async_remote_copy(
@@ -281,7 +295,16 @@
     def wait_sums(phase):
         others = sum_recv.at[phase, pl.ds(0, n - 1)]
         pltpu.make_async_copy(others, others, sum_rsem.at[phase]).wait()
-        return jnp.sum(sum_recv[phase], axis=0)
+        if n > 64:
+            return jnp.sum(sum_recv[phase], axis=0)
+        parts = [sum_recv[phase, i] for i in range(n)]
+        while len(parts) > 1:
+            odd = parts[len(parts) // 2 * 2 :]
+            parts = [a + b for a, b in zip(parts[::2], parts[1::2])] + odd
+        return parts[0]
+
+    def spread(row, at):
+        return jnp.broadcast_to(row[:, at : at + 1], (1, lanes))
 
     def total_row(blocks, sums):
         if sums:
@@ -383,18 +406,24 @@
 
     pl.when(above)(hear_and_send)
 
-    wait_edges(0, EVERY)
-    visc_halo = [edge_recv[0, d, 2 * comps : 2 * comps + 1] for d in range(2)]
-    for d in (EAST, WEST):
-        visc_halo.append(row_to_cols(edge_recv[0, d, 2:3])[0])
-    faces = [0.5 * (visc + v) for v in shifted(visc, *visc_halo)]
+    wait_edges(0, (EAST, WEST))
+    sides = [row_to_cols(edge_recv[0, d, 2:3])[0] for d in (EAST, WEST)]
+    _, below_visc, *beside = shifted(visc, 0.0, 0.0, *sides)
+    open_north = 1.0 + 0.5 * (visc + below_visc)
+    for v in beside:
+        open_north = open_north + 0.5 * (visc + v)
+    edge_send[1, NORTH, 0:1] = open_north[rows - 1 : rows]
+    send_edges(1, (NORTH,))
+
+    wait_edges(0, (NORTH, SOUTH))
+    visc_halo = [edge_recv[0, d, 2 * comps : 2 * comps + 1] for d in (NORTH, SOUTH)]
+    faces = [0.5 * (visc + v) for v in shifted(visc, *visc_halo, *sides)]
     diagonal = 1.0 + faces[0] + faces[1] + faces[2] + faces[3]
     inverse = 1.0 / diagonal
     scaled = [u * inverse for u in free]
     jacobi = [s + (1.0 - u) for s, u in zip(scaled, free)]
-    for d in (NORTH, EAST):
-        put_edge(1, d, scaled, 0)
-    send_edges(1, (NORTH, EAST))
+    put_edge(1, EAST, scaled, 0)
+    send_edges(1, (EAST,))
 
     pl.when(has[SOUTH])(row_copy.wait_recv)
     pl.when(has[WEST])(col_copy.wait_recv)
@@ -404,16 +433,25 @@
     wait_edges(1, (SOUTH, WEST))
     south_right = [edge_recv[0, SOUTH, c : c + 1] for c in range(comps)]
     south_free = [edge_recv[0, SOUTH, comps + c : comps + c + 1] for c in range(comps)]
-    south_scaled = [edge_recv[1, SOUTH, c : c + 1] for c in range(comps)]
+    south_inverse = 1.0 / jnp.where(
+        has[SOUTH], edge_recv[1, SOUTH, 0:1] + faces[1][0:1], 1.0
+    )
+    south_scaled = [u * south_inverse for u in south_free]
     west_right, west_free = edge_recv[0, WEST, 0:1], edge_recv[0, WEST, 1:2]
     west_scaled = edge_recv[1, WEST, 0:1]
 
-    def operate(x, coeffs, south_res, west_res):
+    def halo_values(lifted, south_res, west_res):
         south = [
-            s * r + u * lift(row_recv[c], coeffs)
-            for c, (s, r, u) in enumerate(zip(south_scaled, south_res, south_free))
+            a * r + u * b
+            for a, r, u, b in zip(south_scaled, south_res, south_free, lifted[0])
         ]
-        west = west_scaled * west_res + west_free * lift(col_recv[...], coeffs)
+        return south, west_scaled * west_res + west_free * lifted[1]
+
+    def lift_halos(coeffs):
+        south = [lift(row_recv[c], coeffs) for c in range(comps)]
+        return south, lift(col_recv[...], coeffs)
+
+    def operate(x, south, west):
         west_cols = row_to_cols(west)
         out, to_south, to_west = [], [], []
         for c in range(comps):
@@ -428,7 +466,7 @@
             out.append(free[c] * stencil + (1.0 - free[c]) * x[c])
             to_south.append(faces[1] * masked)
             to_west.append(faces[3] * masked)
-        return out, to_south, to_west, south, west
+        return out, to_south, to_west
 
     def put_terms(stage, to_south, to_west):
         south_rows = edge_rows(SOUTH, to_south)
@@ -461,10 +499,10 @@
 
     dot = wait_sums(0)
     coeffs = solve(dot)
-    direction = [j * r + b for j, r, b in zip(jacobi, right, lift_all(coeffs))]
-    image, to_south, to_west, south, west = operate(
-        direction, coeffs, south_right, west_right
-    )
+    lifted, lifted_halos = lift_all(coeffs), lift_halos(coeffs)
+    direction = [j * r + b for j, r, b in zip(jacobi, right, lifted)]
+    south, west = halo_values(lifted_halos, south_right, west_right)
+    image, to_south, to_west = operate(direction, south, west)
     south_term, west_term = put_terms(2, to_south, to_west)
     across = project(image)
     extra = col_recv[...] * west_term
@@ -505,18 +543,24 @@
     ]
     west_image = edge_recv[2, WEST, 0:1] + west_term - west_free * diag_recv[1, 0:1]
     sums = wait_sums(1)
-    energy = sums[:, basis : basis + 1]
-    curve = sums[:, basis + 1 : basis + 2]
+    energy, curve = spread(sums, basis), spread(sums, basis + 1)
     step = energy / curve
+    coeffs = solve(sums)
     residual = [r - step * w for r, w in zip(right, image)]
-    coeffs = solve(dot - step * sums)
-    smoothed = [j * r + b for j, r, b in zip(jacobi, residual, lift_all(coeffs))]
-    smoothed_image, to_south, to_west, south, west = operate(
-        smoothed,
-        coeffs,
+    smoothed = [
+        j * r + (b - step * l)
+        for j, r, b, l in zip(jacobi, residual, lifted, lift_all(coeffs))
+    ]
+    south_lift, west_lift = lift_halos(coeffs)
+    south, west = halo_values(
+        (
+            [b - step * l for b, l in zip(lifted_halos[0], south_lift)],
+            lifted_halos[1] - step * west_lift,
+        ),
         [r - step * w for r, w in zip(south_right, south_image)],
         west_right - step * west_image,
     )
+    smoothed_image, to_south, to_west = operate(smoothed, south, west)
     south_term, west_term = put_terms(3, to_south, to_west)
     third = total_row(
         [],
@@ -532,27 +576,26 @@
     send_edges(3, (SOUTH, WEST))
     wait_edges(3, (NORTH, EAST))
     smoothed_image = complete(3, smoothed_image)
+    for phase in range(2):
+        drain_sums(phase)
+    for stage in range(3):
+        drain_edges(stage)
+    for i in range(2):
+        pl.when(has_diag[i])(diag_copy(i).wait_send)
+    pl.when(has[NORTH])(row_copy.wait_send)
+    pl.when(has[EAST])(col_copy.wait_send)
+    pltpu.make_async_copy(others, others, gram_ssem).wait()
     sums = wait_sums(2)
-    energy_new = sums[:, 0:1]
+    energy_new = spread(sums, 0)
     ratio = energy_new / energy
-    curve_new = sums[:, 2:3] + ratio * (2.0 * sums[:, 1:2] + ratio * curve)
+    curve_new = spread(sums, 2) + ratio * (2.0 * spread(sums, 1) + ratio * curve)
     step_new = energy_new / curve_new
     for c in range(comps):
         out_ref[c] = step * direction[c] + step_new * (smoothed[c] + ratio * direction[c])
         out_ref[comps + c] = residual[c] - step_new * (smoothed_image[c] + ratio * image[c])
 
-    for phase in range(3):
-        sent = sum_recv.at[phase, pl.ds(0, n - 1)]
-        pltpu.make_async_copy(sent, sent, sum_ssem.at[phase]).wait()
-    others = gram_full.at[pl.ds(0, ncol - 1)]
-    pltpu.make_async_copy(others, others, gram_ssem).wait()
-    for stage, ways in enumerate((EVERY, (NORTH, EAST), EVERY, (SOUTH, WEST))):
-        for d in ways:
-            pl.when(has[d])(edge_copy(stage, d).wait_send)
-    for i in range(2):
-        pl.when(has_diag[i])(diag_copy(i).wait_send)
-    pl.when(has[NORTH])(row_copy.wait_send)
-    pl.when(has[EAST])(col_copy.wait_send)
+    drain_sums(2)
+    drain_edges(3)
 
 
 def on_device(nrow, ncol, right_side, viscosity, free_mask, coarse_basis, gram_inverse):
@@ -590,8 +633,8 @@
             dma,
             dma,
             dma,
-            dma((4, 4)),
-            dma((4, 4)),
+            dma((len(SENT_AT),)),
+            dma((len(SENT_AT),)),
             dma((2,)),
             dma((2,)),
             dma,

time: 22.9 us -> 22.1 us (0.965)
  Pallas kernels: 21.5 us -> 20.6 us
    pallas_call x1, Pallas kernels: 21.5 us -> 20.6 us  [on_device(): pl.pallas_call(functools.partial(kernel, nrow, ncol, scale), out_shape=pl...]
where the time goes in v3:
time: 22.1 us; the launch traced here: 21.9 us
  Pallas kernels  20.6 us (93%)
  between operations  0.64 us (3%)
  local copies, waits for them, and re-layouts  0.61 us (3%)
    pallas_call x1, Pallas kernels, on_device(): pl.pallas_call(functools.partial(kernel, nrow, ncol, scale), out_shape=pl...  20.6 us
    slice x1, local copies, waits for them, and re-layouts, on_device(): return (out[:comps], out[comps:])  0.61 us

profile of v3, /device:TPU:0, one launch (start us, length us, event | category | flops | bytes accessed | tf_op | source)
XLA Modules:
  0.0 21.9 jit_solution(3469122718027089668)
XLA Ops:
  0.6 20.6 %shard_map.68 = f32[6,8,128]{2,1,0:T(8,128)S(1)} custom-call(f32[3,8,128]{2,1,0:T(8,128)} %r_hbm.1, f32[8,128]{1,0:T(8,128)} %visc_hbm.1, s32[3,8,128]{2,1,0:T(8,128)} %mask_hbm.1, f32[64,3,8,128]{3,2,1,0:T(8,128)} %basis_ref.1, f32[16,64]{1,0:T(8,128)} %gram_hbm.1), custom_call_target="tpu_custom_call" | custom-call | tf_op jit(solution)/shard_map/pallas_call | solution.py:609
  21.3 0.6 %fusion = (f32[3,8,128]{2,1,0:T(8,128)}, f32[3,8,128]{2,1,0:T(8,128)}) fusion(f32[6,8,128]{2,1,0:T(8,128)S(1)} %shard_map.68), kind=kLoop, calls=%fused_computation | loop fusion | bytes 49152 | tf_op jit(solution)/shard_map/slice | solution.py:650

commit v4 on v3

--- a/solution.py
+++ b/solution.py
@@ -116,17 +116,25 @@
 
     barrier = pltpu.get_barrier_semaphore()
 
+    def target(dr, dc):
+        return lax.rem(my_row + dr, nrow), lax.rem(my_col + dc, ncol)
+
     def to_all(act):
+        if n <= 64:
+            rows_to = [lax.rem(my_row + dr, nrow) for dr in range(nrow)]
+            cols_to = [lax.rem(my_col + dc, ncol) for dc in range(ncol)]
+            for dr in zigzag(nrow) + [0]:
+                for dc in zigzag(ncol) + [0]:
+                    if dr or dc:
+                        act((rows_to[dr], cols_to[dc]))
+            return
+
         def one(i, carry):
             t = lax.rem(me + i, n)
             act((t // ncol, lax.rem(t, ncol)))
             return carry
 
-        if n <= 64:
-            for i in zigzag(n):
-                one(i, 0)
-        else:
-            lax.fori_loop(1, n, one, 0)
+        lax.fori_loop(1, n, one, 0)
 
     depth = plane_rows(nrow)
     planes = nrow // depth
@@ -222,7 +230,7 @@
         return pltpu.make_async_remote_copy(
             src_ref=edge_send.at[stage, d],
             dst_ref=edge_recv.at[stage, OPPOSITE[d]],
-            send_sem=edge_ssem.at[SENT_AT[stage, d]],
+            send_sem=edge_ssem.at[d],
             recv_sem=edge_rsem.at[SENT_AT[stage, d]],
             device_id=where_to[d],
             device_id_type=MESH,
@@ -233,19 +241,20 @@
         return pltpu.make_async_remote_copy(
             src_ref=edge_send.at[stage, d],
             dst_ref=edge_recv.at[stage, d],
-            send_sem=edge_ssem.at[at],
+            send_sem=edge_ssem.at[OPPOSITE[d]],
             recv_sem=edge_rsem.at[at],
             device_id=where_to[d],
             device_id_type=MESH,
         )
 
-    def drain_sums(phase):
-        sent = sum_recv.at[phase, pl.ds(0, n - 1)]
-        pltpu.make_async_copy(sent, sent, sum_ssem.at[phase]).wait()
-
-    def drain_edges(stage):
-        for d in SENT[stage]:
-            pl.when(has[d])(edge_copy(stage, d).wait_send)
+    def drain_sums():
+        sent = sum_recv.at[:, pl.ds(0, n - 1)]
+        pltpu.make_async_copy(sent, sent, sum_ssem).wait()
+
+    def drain_edges():
+        for d in EVERY:
+            sent = edge_send.at[0, pl.ds(0, sum(d in ways for ways in SENT))]
+            pl.when(has[d])(pltpu.make_async_copy(sent, sent, edge_ssem.at[d]).wait)
 
     def diag_copy(i):
         return pltpu.make_async_remote_copy(
@@ -285,7 +294,7 @@
             lambda device: pltpu.make_async_remote_copy(
                 src_ref=sum_send.at[phase],
                 dst_ref=sum_recv.at[phase, me],
-                send_sem=sum_ssem.at[phase],
+                send_sem=sum_ssem,
                 recv_sem=sum_rsem.at[phase],
                 device_id=device,
                 device_id_type=MESH,
@@ -576,10 +585,6 @@
     send_edges(3, (SOUTH, WEST))
     wait_edges(3, (NORTH, EAST))
     smoothed_image = complete(3, smoothed_image)
-    for phase in range(2):
-        drain_sums(phase)
-    for stage in range(3):
-        drain_edges(stage)
     for i in range(2):
         pl.when(has_diag[i])(diag_copy(i).wait_send)
     pl.when(has[NORTH])(row_copy.wait_send)
@@ -594,8 +599,8 @@
         out_ref[c] = step * direction[c] + step_new * (smoothed[c] + ratio * direction[c])
         out_ref[comps + c] = residual[c] - step_new * (smoothed_image[c] + ratio * image[c])
 
-    drain_sums(2)
-    drain_edges(3)
+    drain_sums()
+    drain_edges()
 
 
 def on_device(nrow, ncol, right_side, viscosity, free_mask, coarse_basis, gram_inverse):
@@ -633,13 +638,13 @@
             dma,
             dma,
             dma,
-            dma((len(SENT_AT),)),
+            dma((4,)),
             dma((len(SENT_AT),)),
             dma((2,)),
             dma((2,)),
             dma,
             dma,
-            dma((3,)),
+            dma,
             dma((3,)),
             pltpu.SemaphoreType.REGULAR,
         ],

time: 22.1 us -> 22 us (level)
  no operation moved by 1% of the time
where the time goes in v4:
time: 22 us; the launch traced here: 21.7 us
  Pallas kernels  20.5 us (93%)
  between operations  0.64 us (3%)
  local copies, waits for them, and re-layouts  0.61 us (3%)
    pallas_call x1, Pallas kernels, on_device(): pl.pallas_call(functools.partial(kernel, nrow, ncol, scale), out_shape=pl...  20.5 us
    slice x1, local copies, waits for them, and re-layouts, on_device(): return (out[:comps], out[comps:])  0.61 us

profile of v4, /device:TPU:0, one launch (start us, length us, event | category | flops | bytes accessed | tf_op | source)
XLA Modules:
  0.0 21.7 jit_solution(9874934053309502061)
XLA Ops:
  0.6 20.5 %shard_map.68 = f32[6,8,128]{2,1,0:T(8,128)S(1)} custom-call(f32[3,8,128]{2,1,0:T(8,128)} %r_hbm.1, f32[8,128]{1,0:T(8,128)} %visc_hbm.1, s32[3,8,128]{2,1,0:T(8,128)} %mask_hbm.1, f32[64,3,8,128]{3,2,1,0:T(8,128)} %basis_ref.1, f32[16,64]{1,0:T(8,128)} %gram_hbm.1), custom_call_target="tpu_custom_call" | custom-call | tf_op jit(solution)/shard_map/pallas_call | solution.py:614
  21.1 0.6 %fusion = (f32[3,8,128]{2,1,0:T(8,128)}, f32[3,8,128]{2,1,0:T(8,128)}) fusion(f32[6,8,128]{2,1,0:T(8,128)S(1)} %shard_map.68), kind=kLoop, calls=%fused_computation | loop fusion | bytes 49152 | tf_op jit(solution)/shard_map/slice | solution.py:655

commit v5 on v4

--- a/solution.py
+++ b/solution.py
@@ -151,15 +151,17 @@
     greeted = plane * group + group - 1 + jnp.where(cross_up, 1, 0)
     pl.when(cross_down)(functools.partial(greet, (my_row - 1, my_col)))
 
+    for dr in zigzag(depth) + [0]:
+        row = plane * depth + lax.rem(spot_row + dr, depth)
+        for dc in zigzag(ncol) + [0]:
+            if dr or dc:
+                greet((row, lax.rem(my_col + dc, ncol)))
     def greet_higher(i, carry):
         t = (plane + 1) * group + i
         greet((t // ncol, lax.rem(t, ncol)))
         return carry
 
     lax.fori_loop(0, (planes - 1 - plane) * group, greet_higher, 0)
-    for i in zigzag(group):
-        t = lax.rem(mine + i, group)
-        greet((plane * depth + t // ncol, lax.rem(t, ncol)))
 
     def tell_lower():
         def tell(q, carry):
@@ -315,14 +317,15 @@
     def spread(row, at):
         return jnp.broadcast_to(row[:, at : at + 1], (1, lanes))
 
-    def total_row(blocks, sums):
-        if sums:
-            pad = jnp.zeros((rows - len(sums), lanes), F32)
-            blocks = blocks + [jnp.concatenate(sums + [pad], axis=0)]
+    def total_row(blocks, tiles):
         out = None
         for i, block in enumerate(blocks):
             col = jnp.sum(block, axis=1, keepdims=True)
             term = jnp.where(lane_of == row_of + i * rows, col, 0.0)
+            out = term if out is None else out + term
+        for i, tile in enumerate(tiles):
+            col = jnp.sum(tile, axis=1, keepdims=True)
+            term = jnp.where(lane_of == len(blocks) * rows + i, col, 0.0)
             out = term if out is None else out + term
         return jnp.sum(out, axis=0, keepdims=True)
 
@@ -346,8 +349,7 @@
     def inner(xs, ys):
         out = None
         for x, y in zip(xs, ys):
-            term = jnp.sum(x * y, axis=0, keepdims=True)
-            out = term if out is None else out + term
+            out = x * y if out is None else out + x * y
         return out
 
     for load in small:
@@ -393,10 +395,10 @@
     tell_lower()
     send_edges(0, EVERY)
     pltpu.make_async_copy(basis_t, basis_t, load_sem).wait()
+    keep_sums(0, total_row(project(right), []))
+
+    pl.when(top)(lambda: send_sums(0))
     pl.when(has[NORTH])(row_copy.start)
-    keep_sums(0, total_row(project(right), []))
-
-    pl.when(top)(lambda: send_sums(0))
     for i in range(1, ncol):
         gram_copy(i).start()
 
@@ -489,7 +491,7 @@
         total = west * west_term
         for a, b in zip(south, south_term):
             total = total + a * b
-        return total
+        return jnp.where(row_of == 0, total, 0.0)
 
     def complete(stage, image):
         east_cols = row_to_cols(edge_recv[stage, EAST, 0:1])

time: 22 us -> 22 us (level)
  no operation moved by 1% of the time
where the time goes in v5:
time: 22 us; the launch traced here: 21.7 us
  Pallas kernels  20.5 us (93%)
  between operations  0.64 us (3%)
  local copies, waits for them, and re-layouts  0.61 us (3%)
    pallas_call x1, Pallas kernels, on_device(): pl.pallas_call(functools.partial(kernel, nrow, ncol, scale), out_shape=pl...  20.5 us
    slice x1, local copies, waits for them, and re-layouts, on_device(): return (out[:comps], out[comps:])  0.61 us

profile of v5, /device:TPU:0, one launch (start us, length us, event | category | flops | bytes accessed | tf_op | source)
XLA Modules:
  0.0 21.7 jit_solution(2233855086440018369)
XLA Ops:
  0.6 20.5 %shard_map.68 = f32[6,8,128]{2,1,0:T(8,128)S(1)} custom-call(f32[3,8,128]{2,1,0:T(8,128)} %r_hbm.1, f32[8,128]{1,0:T(8,128)} %visc_hbm.1, s32[3,8,128]{2,1,0:T(8,128)} %mask_hbm.1, f32[64,3,8,128]{3,2,1,0:T(8,128)} %basis_ref.1, f32[16,64]{1,0:T(8,128)} %gram_hbm.1), custom_call_target="tpu_custom_call" | custom-call | tf_op jit(solution)/shard_map/pallas_call | solution.py:616
  21.1 0.6 %fusion = (f32[3,8,128]{2,1,0:T(8,128)}, f32[3,8,128]{2,1,0:T(8,128)}) fusion(f32[6,8,128]{2,1,0:T(8,128)S(1)} %shard_map.68), kind=kLoop, calls=%fused_computation | loop fusion | bytes 49152 | tf_op jit(solution)/shard_map/slice | solution.py:657

commit v6 on v5

--- a/solution.py
+++ b/solution.py
@@ -166,7 +166,7 @@
     def tell_lower():
         def tell(q, carry):
             pl.semaphore_signal(
-                chain_sem,
+                chain_sem.at[plane],
                 inc=1,
                 device_id=(q * depth + spot_row, my_col),
                 device_id_type=MESH,
@@ -174,9 +174,6 @@
             return carry
 
         lax.fori_loop(0, plane, tell, 0)
-
-    def hear_higher():
-        pl.when(above)(lambda: pl.semaphore_wait(chain_sem, planes - 1 - plane))
 
     top = jnp.logical_not(above)
 
@@ -291,17 +288,18 @@
         sum_send[phase] = row
         sum_recv[phase, me] = row
 
+    def send_to(phase, device):
+        pltpu.make_async_remote_copy(
+            src_ref=sum_send.at[phase],
+            dst_ref=sum_recv.at[phase, me],
+            send_sem=sum_ssem,
+            recv_sem=sum_rsem.at[phase],
+            device_id=device,
+            device_id_type=MESH,
+        ).start()
+
     def send_sums(phase):
-        to_all(
-            lambda device: pltpu.make_async_remote_copy(
-                src_ref=sum_send.at[phase],
-                dst_ref=sum_recv.at[phase, me],
-                send_sem=sum_ssem,
-                recv_sem=sum_rsem.at[phase],
-                device_id=device,
-                device_id_type=MESH,
-            ).start()
-        )
+        to_all(functools.partial(send_to, phase))
 
     def wait_sums(phase):
         others = sum_recv.at[phase, pl.ds(0, n - 1)]
@@ -411,9 +409,26 @@
     col_send[...] = column
     pl.when(has[EAST])(col_copy.start)
 
+    def send_plane(q):
+        for dr in zigzag(depth) + [0]:
+            row = q * depth + lax.rem(spot_row + dr, depth)
+            for dc in zigzag(ncol) + [0]:
+                send_to(0, (row, lax.rem(my_col + dc, ncol)))
+
     def hear_and_send():
-        hear_higher()
-        send_sums(0)
+        for dr in zigzag(depth) + [0]:
+            row = plane * depth + lax.rem(spot_row + dr, depth)
+            for dc in zigzag(ncol) + [0]:
+                if dr or dc:
+                    send_to(0, (row, lax.rem(my_col + dc, ncol)))
+        for q in range(planes - 1):
+            pl.when(q < plane)(functools.partial(send_plane, q))
+        for q in range(1, planes):
+
+            @pl.when(q > plane)
+            def _(q=q):
+                pl.semaphore_wait(chain_sem.at[q], 1)
+                send_plane(q)
 
     pl.when(above)(hear_and_send)
 
@@ -648,7 +663,7 @@
             dma,
             dma,
             dma((3,)),
-            pltpu.SemaphoreType.REGULAR,
+            pltpu.SemaphoreType.REGULAR((nrow // plane_rows(nrow),)),
         ],
         compiler_params=pltpu.CompilerParams(
             collective_id=0, has_side_effects=True, vmem_limit_bytes=60_000_000

time: 22 us -> 21.9 us (level)
  no operation moved by 1% of the time
where the time goes in v6:
time: 21.9 us; the launch traced here: 21.7 us
  Pallas kernels  20.4 us (93%)
  between operations  0.64 us (3%)
  local copies, waits for them, and re-layouts  0.61 us (3%)
    pallas_call x1, Pallas kernels, on_device(): pl.pallas_call(functools.partial(kernel, nrow, ncol, scale), out_shape=pl...  20.4 us
    slice x1, local copies, waits for them, and re-layouts, on_device(): return (out[:comps], out[comps:])  0.61 us

profile of v6, /device:TPU:0, one launch (start us, length us, event | category | flops | bytes accessed | tf_op | source)
XLA Modules:
  0.0 21.7 jit_solution(4087937553613930499)
XLA Ops:
  0.6 20.4 %shard_map.68 = f32[6,8,128]{2,1,0:T(8,128)S(1)} custom-call(f32[3,8,128]{2,1,0:T(8,128)} %r_hbm.1, f32[8,128]{1,0:T(8,128)} %visc_hbm.1, s32[3,8,128]{2,1,0:T(8,128)} %mask_hbm.1, f32[64,3,8,128]{3,2,1,0:T(8,128)} %basis_ref.1, f32[16,64]{1,0:T(8,128)} %gram_hbm.1), custom_call_target="tpu_custom_call" | custom-call | tf_op jit(solution)/shard_map/pallas_call | solution.py:631
  21.1 0.6 %fusion = (f32[3,8,128]{2,1,0:T(8,128)}, f32[3,8,128]{2,1,0:T(8,128)}) fusion(f32[6,8,128]{2,1,0:T(8,128)S(1)} %shard_map.68), kind=kLoop, calls=%fused_computation | loop fusion | bytes 49152 | tf_op jit(solution)/shard_map/slice | solution.py:672
